TPU v7x, 32 devices: a 4x2x2 block of a 4x4x8 slice. The times are simulated.
32 devices in a mesh: dp: 4 (over y, z), sp: 8 (over x, core).
Axes of the slice: x: 4, y: 2, z: 2, core: 2. Of those that a mesh axis runs over, the one named last changes fastest.
The devices are a block of a 4x4x8 slice.
Arguments:
- resid_x: bfloat16 [64, 1024, 2048], P('dp', 'sp'), parts along dimension 0
- positions: int32 [64, 1024], P('dp', 'sp'), parts along dimension 0
- w_query: bfloat16 [2048, 2048], replicated
- w_key: bfloat16 [2048, 2048], replicated
- w_value: bfloat16 [2048, 2048], replicated
- w_out: bfloat16 [2048, 2048], replicated
- gain_q: bfloat16 [2048], replicated
- gain_k: bfloat16 [2048], replicated
- gain_out: bfloat16 [2048], replicated
Outputs:
- output: bfloat16 [64, 1024, 2048], P('dp', 'sp'), parts along dimension 0
There are 4 independent parts. A program takes and returns all parts, laid end to end along the dimension named above; an argument that names none is the same for every part.
All inputs are finite; a program needn't handle non-finite values.
Results may differ from a plain program's by a relative error of at most 0.0179203.
Values are sent between devices in bfloat16 or wider.
A program may use at most 768 MiB of HBM per device.

v0:
```python
import jax
import jax.numpy as jnp
from jax import lax
from jax.sharding import PartitionSpec as P

HEAD_DIM = 128
QUERY_BLOCKS = 8
ROPE_THETA = 500000.0
NORM_EPS = 1e-6
SCALE = HEAD_DIM ** -0.5


def rope_tables(pos_ids):
    inv_freq = 1.0 / (ROPE_THETA ** (jnp.arange(0, HEAD_DIM, 2, dtype=jnp.float32) / HEAD_DIM))
    angles = pos_ids.astype(jnp.float32)[..., None] * inv_freq
    return jnp.cos(angles), jnp.sin(angles)


def apply_rope(heads_f32, cos_t, sin_t):
    half = HEAD_DIM // 2
    cos_b = cos_t[:, :, None, :]
    sin_b = sin_t[:, :, None, :]
    first = heads_f32[..., :half]
    second = heads_f32[..., half:]
    return jnp.concatenate([first * cos_b - second * sin_b, second * cos_b + first * sin_b], axis=-1)


def rms_scale(vals_f32, gain):
    mean_sq = jnp.mean(vals_f32 * vals_f32, axis=-1, keepdims=True)
    return vals_f32 * lax.rsqrt(mean_sq + NORM_EPS) * gain.astype(jnp.float32)


def project(x_tok, weight):
    return jnp.einsum('bsd,de->bse', x_tok, weight, preferred_element_type=jnp.float32).astype(jnp.bfloat16)


def norm_rope(x_tok, weight, gain, cos_t, sin_t):
    proj = project(x_tok, weight).astype(jnp.float32)
    batch, seq_len, model_width = proj.shape
    normed = rms_scale(proj, gain).reshape(batch, seq_len, model_width // HEAD_DIM, HEAD_DIM)
    return apply_rope(normed, cos_t, sin_t).astype(jnp.bfloat16)


def causal_attention(q_heads, k_heads, v_heads):
    seq_len = q_heads.shape[1]
    block = seq_len // QUERY_BLOCKS
    outs = []
    for blk_idx in range(QUERY_BLOCKS):
        key_end = (blk_idx + 1) * block
        q_blk = q_heads[:, blk_idx * block:key_end]
        scores = jnp.einsum('bqhd,bkhd->bhqk', q_blk, k_heads[:, :key_end], preferred_element_type=jnp.float32) * SCALE
        q_idx = blk_idx * block + jnp.arange(block)
        scores = jnp.where(jnp.arange(key_end)[None, :] <= q_idx[:, None], scores, -1e30)
        probs = jax.nn.softmax(scores, axis=-1).astype(jnp.bfloat16)
        outs.append(jnp.einsum('bhqk,bkhd->bqhd', probs, v_heads[:, :key_end], preferred_element_type=jnp.float32).astype(jnp.bfloat16))
    return jnp.concatenate(outs, axis=1)


def solution(mesh):
    def local_block(x_loc, pos_loc, w_query, w_key, w_value, w_out, gain_q, gain_k, gain_out):
        batch, seq_loc, model_width = x_loc.shape
        cos_t, sin_t = rope_tables(pos_loc)
        q_loc = norm_rope(x_loc, w_query, gain_q, cos_t, sin_t)
        k_loc = norm_rope(x_loc, w_key, gain_k, cos_t, sin_t)
        v_loc = project(x_loc, w_value).reshape(batch, seq_loc, model_width // HEAD_DIM, HEAD_DIM)
        q_heads = lax.all_to_all(q_loc, 'sp', 2, 1, tiled=True)
        k_heads = lax.all_to_all(k_loc, 'sp', 2, 1, tiled=True)
        v_heads = lax.all_to_all(v_loc, 'sp', 2, 1, tiled=True)
        o_heads = causal_attention(q_heads, k_heads, v_heads)
        o_loc = lax.all_to_all(o_heads, 'sp', 1, 2, tiled=True).reshape(batch, seq_loc, model_width)
        attn_out = project(o_loc, w_out).astype(jnp.float32)
        return (x_loc.astype(jnp.float32) + rms_scale(attn_out, gain_out)).astype(jnp.bfloat16)

    tok_spec = P('dp', 'sp', None)
    return jax.shard_map(local_block, mesh=mesh, in_specs=(tok_spec, P('dp', 'sp'), P(), P(), P(), P(), P(), P(), P()), out_specs=tok_spec, check_vma=False)
```

profile of v0, /device:TPU:81, one launch (start us, length us, event | category | flops | bytes accessed | tf_op | source)
XLA Modules:
  0.0 817.9 jit_solution(214038374929833336)
XLA Ops:
  0.0 0.6 negate_power_fusion
  0.6 23.6 %fusion.8 = (f32[16,128]{1,0:T(8,128)S(1)}, bf16[16,128,2048]{2,1,0:T(8,128)(2,1)}) fusion(bf16[16,128,2048]{2,1,0:T(8,128)(2,1)} %param.9, bf16[2048,2048]{1,0:T(8,128)(2,1)} %param.11), kind=kOutput, calls=%fused_computation.14 | convolution fusion | flops 17196644352 | bytes 25174016 | tf_op jit(solution)/shard_map/bsd,de->bse/dot_general | solution.py:34
  24.2 0.0 copy-done.2
  24.2 0.0 slice-start.7
  24.2 11.0 %fusion.9 = f32[16,128,2048]{2,1,0:T(8,128)} fusion(bf16[16,128,2048]{2,1,0:T(8,128)(2,1)} %get-tuple-element.18, f32[2048]{0:T(1024)S(1)} %convert_element_type.117, f32[16,128]{1,0:T(8,128)S(1)} %add_rsqrt_fusion.2), kind=kLoop, calls=%fused_computation.15 | loop fusion | flops 12582912 | bytes 25182208 | tf_op jit(solution)/shard_map/mul | solution.py:30
  35.2 14.3 %copy.32 = f32[256,8,16,128]{3,2,1,0:T(8,128)} copy(f32[256,8,16,128]{3,1,2,0:T(8,128)} %bitcast.107) | data formatting | bytes 33554432
  49.5 0.0 slice-done.7
  49.5 22.2 %fusion.10 = (f32[16,128]{1,0:T(8,128)S(1)}, bf16[16,128,2048]{2,1,0:T(8,128)(2,1)}) fusion(bf16[16,128,2048]{2,1,0:T(8,128)(2,1)S(1)} %bitcast.133, bf16[2048,2048]{1,0:T(8,128)(2,1)} %param.12), kind=kOutput, calls=%fused_computation.16 | convolution fusion | flops 17196644352 | bytes 25174016 | tf_op jit(solution)/shard_map/bsd,de->bse/dot_general | solution.py:34
  71.7 10.8 %fusion.11 = f32[16,128,2048]{2,1,0:T(8,128)} fusion(bf16[16,128,2048]{2,1,0:T(8,128)(2,1)} %get-tuple-element.20, f32[2048]{0:T(1024)S(1)} %convert_element_type.121, f32[16,128]{1,0:T(8,128)S(1)} %add_rsqrt_fusion.1), kind=kLoop, calls=%fused_computation.17 | loop fusion | flops 12582912 | bytes 25182208 | tf_op jit(solution)/shard_map/mul | solution.py:30
  82.6 14.1 %copy.33 = f32[256,8,16,128]{3,2,1,0:T(8,128)} copy(f32[256,8,16,128]{3,1,2,0:T(8,128)} %bitcast.108) | data formatting | bytes 33554432
  96.7 45.6 %fusion.200 = (f32[16,128,16,64]{3,2,1,0:T(8,128)}, f32[16,128,16,64]{3,2,1,0:T(8,128)}, f32[16,128,16,64]{3,2,1,0:T(8,128)}, f32[16,128,16,64]{3,2,1,0:T(8,128)}) fusion(f32[16,128,16,128]{3,2,1,0:T(8,128)} %bitcast.105, f32[16,128,16,128]{3,2,1,0:T(8,128)} %bitcast.106), kind=kLoop, calls=%fused_computation.202 | loop fusion | bytes 67108864 | tf_op jit(solution)/shard_map/slice | solution.py:23
  142.3 3.7 multiply_cosine_fusion
  146.0 52.6 %subtract_convert_fusion.1 = (bf16[16,128,16,64]{3,1,0,2:T(8,128)(2,1)}, bf16[16,128,16,64]{3,1,0,2:T(8,128)(2,1)}, bf16[16,128,16,64]{3,1,0,2:T(8,128)(2,1)}, bf16[16,128,16,64]{3,1,0,2:T(8,128)(2,1)}) fusion(f32[16,128,16,64]{3,2,1,0:T(8,128)} %get-tuple-element.10, f32[16,128,16,64]{3,2,1,0:T(8,128)} %get-tuple-element.9, ...), kind=kLoop, calls=%fused_computation.28 | loop fusion | flops 33554432 | bytes 51380224 | tf_op jit(solution)/shard_map/convert.2
  198.6 11.4 %pad_maximum_fusion = bf16[16,128,16,128]{3,1,0,2:T(8,128)(2,1)} fusion(bf16[16,128,16,64]{3,1,0,2:T(8,128)(2,1)} %get-tuple-element.6, bf16[16,128,16,64]{3,1,0,2:T(8,128)(2,1)} %get-tuple-element.5), kind=kLoop, calls=%fused_computation.42 | loop fusion | flops 16777216 | bytes 16777216 | tf_op jit(solution)/shard_map/concatenate | solution.py:25
  210.0 6.9 all-to-all-start.1
  216.9 10.9 %pad_maximum_fusion.1 = bf16[16,128,16,128]{3,1,0,2:T(8,128)(2,1)} fusion(bf16[16,128,16,64]{3,1,0,2:T(8,128)(2,1)} %get-tuple-element.13, bf16[16,128,16,64]{3,1,0,2:T(8,128)(2,1)} %get-tuple-element.14), kind=kLoop, calls=%fused_computation.43 | loop fusion | flops 16777216 | bytes 16777216 | tf_op jit(solution)/shard_map/concatenate | solution.py:25
  227.8 82.7 %all-to-all-done.1 = bf16[16,128,16,128]{3,1,0,2:T(8,128)(2,1)} async-done(((bf16[16,128,16,128]{3,1,0,2:T(8,128)(2,1)}), bf16[16,128,16,128]{3,1,0,2:T(8,128)(2,1)}, u32[]{:S(2)}, u32[]{:S(2)}) %all-to-all-start.1) | async-done | bytes 8388640 | tf_op jit(solution)/shard_map/all_to_all | solution.py:66
  310.5 6.0 all-to-all-start.2
  316.5 23.5 %convert_bitcast_fusion = bf16[16,16,16,8,128]{4,3,2,1,0:T(8,128)(2,1)} fusion(bf16[16,128,2048]{2,1,0:T(8,128)(2,1)} %param.9, bf16[2048,2048]{1,0:T(8,128)(2,1)} %param.13), kind=kOutput, calls=%fused_computation.58 | convolution fusion | flops 17184063488 | bytes 25165824 | tf_op jit(solution)/shard_map/bsd,de->bse/dot_general | solution.py:34
  340.0 9.0 %copy.44 = bf16[16,16,16,8,128]{4,3,1,0,2:T(8,128)(2,1)} copy(bf16[16,16,16,8,128]{4,3,2,1,0:T(8,128)(2,1)} %convert_bitcast_fusion) | data formatting | bytes 16777216 | tf_op jit(solution)/shard_map/reshape | solution.py:65
  349.0 61.0 %all-to-all-done.2 = bf16[16,128,16,128]{3,1,0,2:T(8,128)(2,1)} async-done(((bf16[16,128,16,128]{3,1,0,2:T(8,128)(2,1)}), bf16[16,128,16,128]{3,1,0,2:T(8,128)(2,1)}, u32[]{:S(2)}, u32[]{:S(2)}) %all-to-all-start.2) | async-done | bytes 8388640 | tf_op jit(solution)/shard_map/all_to_all | solution.py:67
  410.1 6.1 all-to-all-start
  416.2 0.1 iota_compare_fusion.6
  416.3 0.1 iota_compare_fusion.5
  416.4 0.1 iota_compare_fusion.4
  416.5 0.1 iota_compare_fusion.3
  416.6 0.1 iota_compare_fusion.2
  416.8 0.1 iota_compare_fusion.1
  416.9 0.1 iota_compare_fusion
  417.0 10.5 %copy.19 = bf16[16,128,8,2,128]{4,1,2,3,0:T(8,128)(2,1)} copy(bf16[16,128,8,2,128]{4,1,0,3,2:T(8,128)(2,1)} %bitcast.5) | data formatting | bytes 16777216 | tf_op jit(solution)/shard_map/all_to_all | solution.py:66
  427.5 10.5 %copy.22 = bf16[16,128,8,2,128]{4,1,2,3,0:T(8,128)(2,1)} copy(bf16[16,128,8,2,128]{4,1,0,3,2:T(8,128)(2,1)} %bitcast.9) | data formatting | bytes 16777216 | tf_op jit(solution)/shard_map/all_to_all | solution.py:67
  438.0 2.5 fusion.202
  440.5 3.7 fusion.156
  444.2 4.7 fusion.83
  448.9 6.4 fusion.76
  455.4 5.8 fusion.68
  461.2 7.1 fusion.60
  468.3 7.9 fusion.42
  476.2 8.8 %fusion.34 = f32[16,2,128,896]{3,2,1,0:T(8,128)} fusion(bf16[16,1024,2,128]{3,1,2,0:T(8,128)(2,1)S(1)} %bitcast.104, bf16[16,1024,2,128]{3,1,2,0:T(8,128)(2,1)} %bitcast.118), kind=kOutput, calls=%fused_computation.64 | convolution fusion | flops 939524096 | bytes 23068672 | tf_op jit(solution)/shard_map/bqhd,bkhd->bhqk/dot_general | solution.py:51
  485.0 11.8 %fusion.213 = (f32[16,2,128]{2,1,0:T(2,128)S(1)}, f32[16,2,128,1024]{3,2,1,0:T(8,128)}) fusion(pred[128,1024]{1,0:T(8,128)(4,1)S(1)} %iota_compare_fusion, bf16[16,1024,2,128]{3,1,2,0:T(8,128)(2,1)} %bitcast.98, bf16[16,1024,2,128]{3,1,2,0:T(8,128)(2,1)} %bitcast.119), kind=kOutput, calls=%fused_computation.211 | convolution fusion | flops 1090520064 | bytes 26361856 | tf_op jit(solution)/shard_map/sub | solution.py:54
  496.8 12.8 %all-to-all-done = bf16[16,128,16,128]{3,1,0,2:T(8,128)(2,1)} async-done(((bf16[16,128,16,128]{3,1,0,2:T(8,128)(2,1)}), bf16[16,128,16,128]{3,1,0,2:T(8,128)(2,1)}, u32[]{:S(2)}, u32[]{:S(2)}) %all-to-all-start) | async-done | bytes 8388640 | tf_op jit(solution)/shard_map/all_to_all | solution.py:68
  509.6 10.5 %copy.16 = bf16[16,128,8,2,128]{4,1,2,3,0:T(8,128)(2,1)} copy(bf16[16,128,8,2,128]{4,1,0,3,2:T(8,128)(2,1)} %bitcast.1) | data formatting | bytes 16777216 | tf_op jit(solution)/shard_map/all_to_all | solution.py:68
  520.1 19.0 %fusion.212 = (f32[16,2,128]{2,1,0:T(2,128)S(1)}, f32[16,2,128,896]{3,2,1,0:T(8,128)}) fusion(f32[16,2,128,896]{3,2,1,0:T(8,128)} %fusion.34, pred[128,896]{1,0:T(8,128)(4,1)S(1)} %iota_compare_fusion.1), kind=kOutput, calls=%fused_computation.210 | output fusion | flops 22020992 | bytes 29491200 | tf_op jit(solution)/shard_map/sub | solution.py:54
  539.1 0.0 slice-start.4
  539.1 16.4 %fusion.211 = (f32[16,2,128]{2,1,0:T(2,128)S(1)}, f32[16,2,128,768]{3,2,1,0:T(8,128)}) fusion(f32[16,2,128,768]{3,2,1,0:T(8,128)} %fusion.42, pred[128,768]{1,0:T(8,128)(4,1)S(1)} %iota_compare_fusion.2), kind=kOutput, calls=%fused_computation.209 | output fusion | flops 18875136 | bytes 25280512 | tf_op jit(solution)/shard_map/sub | solution.py:54
  555.6 7.2 fusion.210
  562.8 12.6 %fusion.209 = (f32[16,2,128]{2,1,0:T(2,128)S(1)}, f32[16,2,128,512]{3,2,1,0:T(8,128)}) fusion(f32[16,2,128,512]{3,2,1,0:T(8,128)} %fusion.68, pred[128,512]{1,0:T(8,128)(4,1)S(1)} %iota_compare_fusion.4), kind=kOutput, calls=%fused_computation.207 | output fusion | flops 12583423 | bytes 16859136 | tf_op jit(solution)/shard_map/sub | solution.py:54
  575.3 9.7 %fusion.208 = (f32[16,2,128]{2,1,0:T(2,128)S(1)}, f32[16,2,128,384]{3,2,1,0:T(8,128)}) fusion(f32[16,2,128,384]{3,2,1,0:T(8,128)} %fusion.76, pred[128,384]{1,0:T(8,128)(4,1)S(1)} %iota_compare_fusion.5), kind=kOutput, calls=%fused_computation.206 | output fusion | flops 9437567 | bytes 12648448 | tf_op jit(solution)/shard_map/sub | solution.py:54
  585.1 3.7 fusion.207
  588.8 3.8 fusion.135
  592.6 4.8 fusion.131
  597.4 5.9 fusion.125
  603.3 5.9 fusion.119
  609.2 6.5 fusion.147
  615.7 9.3 %fusion.113 = bf16[16,1024,2,128]{3,1,2,0:T(8,128)(2,1)} fusion(bf16[16,1024,2,128]{3,1,2,0:T(8,128)(2,1)} %fusion.147, bf16[16,1024,2,128]{3,1,2,0:T(8,128)(2,1)} %bitcast.125, f32[16,2,128,768]{3,2,1,0:T(8,128)} %get-tuple-element.30, f32[16,2,128]{2,1,0:T(2,128)S(1)} %get-tuple-element.29), kind=kOutput, calls=%fused_computation.132 | convolution fusion | flops 812122112 | bytes 19939328 | tf_op jit(solution)/shard_map/bhqk,bkhd->bqhd/dot_general | solution.py:55
  625.0 10.5 %fusion.141 = bf16[16,1024,2,128]{3,1,2,0:T(8,128)(2,1)} fusion(bf16[16,1024,2,128]{3,1,2,0:T(8,128)(2,1)} %fusion.113, bf16[16,1024,2,128]{3,1,2,0:T(8,128)(2,1)} %bitcast.126, f32[16,2,128,896]{3,2,1,0:T(8,128)} %get-tuple-element.32, f32[16,2,128]{2,1,0:T(2,128)S(1)} %get-tuple-element.31), kind=kOutput, calls=%fused_computation.144 | convolution fusion | flops 947388416 | bytes 23085056 | tf_op jit(solution)/shard_map/bhqk,bkhd->bqhd/dot_general | solution.py:55
  635.5 11.6 %fusion.137 = bf16[16,1024,2,128]{3,1,2,0:T(8,128)(2,1)} fusion(bf16[16,1024,2,128]{3,1,2,0:T(8,128)(2,1)} %fusion.141, bf16[16,1024,2,128]{3,1,2,0:T(8,128)(2,1)} %bitcast.127, f32[16,2,128,1024]{3,2,1,0:T(8,128)} %get-tuple-element.34, f32[16,2,128]{2,1,0:T(2,128)S(1)} %get-tuple-element.33), kind=kOutput, calls=%fused_computation.142 | convolution fusion | flops 1082654720 | bytes 26230784 | tf_op jit(solution)/shard_map/bhqk,bkhd->bqhd/dot_general | solution.py:55
  647.1 16.4 %copy.24 = bf16[16,1024,2,128]{3,2,0,1:T(2,128)(2,1)} copy(bf16[16,1024,2,128]{3,1,2,0:T(8,128)(2,1)} %fusion.137) | data formatting | bytes 16777216 | tf_op jit(solution)/shard_map/concatenate | solution.py:56
  663.4 6.5 all-to-all-start.3
  669.9 93.5 %all-to-all-done.3 = bf16[16,1024,2,128]{3,2,0,1:T(2,128)(2,1)} async-done(((bf16[16,1024,2,128]{3,2,0,1:T(2,128)(2,1)}), bf16[16,1024,2,128]{3,2,0,1:T(2,128)(2,1)}, u32[]{:S(2)}, u32[]{:S(2)}) %all-to-all-start.3) | async-done | bytes 8388640 | tf_op jit(solution)/shard_map/all_to_all | solution.py:70
  763.4 8.0 copy.45
  771.4 14.4 %reshape.97 = bf16[16,128,2048]{2,1,0:T(8,128)(2,1)} reshape(bf16[16,128,8,2,128]{4,3,2,1,0:T(2,128)(2,1)} %bitcast.110) | data formatting | bytes 16777216 | tf_op jit(solution)/shard_map/reshape | solution.py:70
  785.8 22.4 %fusion.12 = (f32[16,128]{1,0:T(8,128)S(1)}, bf16[16,128,2048]{2,1,0:T(8,128)(2,1)S(1)}) fusion(bf16[16,128,2048]{2,1,0:T(8,128)(2,1)} %reshape.97, bf16[2048,2048]{1,0:T(8,128)(2,1)} %param.14), kind=kOutput, calls=%fused_computation.18 | convolution fusion | flops 17196644352 | bytes 25174016 | tf_op jit(solution)/shard_map/bsd,de->bse/dot_general | solution.py:34
  808.1 9.3 %fusion.15 = bf16[16,128,2048]{2,1,0:T(8,128)(2,1)} fusion(bf16[16,128,2048]{2,1,0:T(8,128)(2,1)S(1)} %get-tuple-element.36, bf16[16,128,2048]{2,1,0:T(8,128)(2,1)} %param.9, f32[2048]{0:T(1024)S(1)} %convert_element_type.148, f32[16,128]{1,0:T(8,128)S(1)} %add_rsqrt_fusion), kind=kLoop, calls=%fused_computation.21 | loop fusion | flops 25165824 | bytes 25182208 | tf_op jit(solution)/shard_map/convert_element_type | solution.py:72
  (45 shorter events, 0.1 us)
Async XLA Ops:
  0.6 23.6 %copy-start.2 = (bf16[2048]{0:T(1024)(128)(2,1)S(1)}, bf16[2048]{0:T(1024)(128)(2,1)}, u32[]{:S(2)}) copy-start(bf16[2048]{0:T(1024)(128)(2,1)} %param.15) | copy-start | bytes 12292
  24.2 25.3 %slice-start.7 = ((s8[8388608]{0:T(1024)(128)(4,1)}), s8[4194304]{0:T(1024)(128)(4,1)S(1)}, s32[]{:S(2)}) async-start(s8[8388608]{0:T(1024)(128)(4,1)} %bitcast.132), calls=%async_computation.11 | async-start | bytes 8388608
  35.2 14.3 %slice-start.8 = ((s8[8388608]{0:T(1024)(128)(4,1)}), s8[4194304]{0:T(1024)(128)(4,1)S(1)}, s32[]{:S(2)}) async-start(s8[8388608]{0:T(1024)(128)(4,1)} %bitcast.132), calls=%async_computation.12 | async-start | bytes 8388608
  49.5 22.2 %copy-start.3 = (bf16[2048]{0:T(1024)(128)(2,1)S(1)}, bf16[2048]{0:T(1024)(128)(2,1)}, u32[]{:S(2)}) copy-start(bf16[2048]{0:T(1024)(128)(2,1)} %param.16) | copy-start | bytes 12292
  82.6 14.1 %copy-start.1 = (s32[16,128]{1,0:T(8,128)S(1)}, s32[16,128]{1,0:T(8,128)}, u32[]{:S(2)}) copy-start(s32[16,128]{1,0:T(8,128)} %param.10) | copy-start | bytes 24580
  96.7 45.6 %copy-start.5 = (f32[64]{0:T(128)S(1)}, f32[64]{0:T(128)}, u32[]{:S(2)}) copy-start(f32[64]{0:T(128)} %negate_power_fusion) | copy-start | bytes 772
  210.0 100.5 %all-to-all-start.1 = ((bf16[16,128,16,128]{3,1,0,2:T(8,128)(2,1)}), bf16[16,128,16,128]{3,1,0,2:T(8,128)(2,1)}, u32[]{:S(2)}, u32[]{:S(2)}) async-start(bf16[16,128,16,128]{3,1,0,2:T(8,128)(2,1)} %pad_maximum_fusion), calls=%async_computation.1 | async-start | bytes 16777216 | tf_op jit(solution)/shard_map/all_to_all | solution.py:66
  310.5 99.6 %all-to-all-start.2 = ((bf16[16,128,16,128]{3,1,0,2:T(8,128)(2,1)}), bf16[16,128,16,128]{3,1,0,2:T(8,128)(2,1)}, u32[]{:S(2)}, u32[]{:S(2)}) async-start(bf16[16,128,16,128]{3,1,0,2:T(8,128)(2,1)} %pad_maximum_fusion.1), calls=%async_computation.2 | async-start | bytes 16777216 | tf_op jit(solution)/shard_map/all_to_all | solution.py:67
  410.1 99.5 %all-to-all-start = ((bf16[16,128,16,128]{3,1,0,2:T(8,128)(2,1)}), bf16[16,128,16,128]{3,1,0,2:T(8,128)(2,1)}, u32[]{:S(2)}, u32[]{:S(2)}) async-start(bf16[16,128,16,128]{3,1,0,2:T(8,128)(2,1)} %bitcast.109), calls=%async_computation | async-start | bytes 16777216 | tf_op jit(solution)/shard_map/all_to_all | solution.py:68
  444.2 11.2 %slice-start = ((s8[8388608]{0:T(1024)(128)(4,1)}), s8[4194304]{0:T(1024)(128)(4,1)S(1)}, s32[]{:S(2)}) async-start(s8[8388608]{0:T(1024)(128)(4,1)} %bitcast.99), calls=%async_computation.4 | async-start | bytes 8388608
  448.9 6.5 slice-start.1
  520.1 35.4 %slice-start.2 = ((s8[10485760]{0:T(1024)(128)(4,1)}), s8[2097152]{0:T(1024)(128)(4,1)S(1)}, s32[]{:S(2)}) async-start(s8[10485760]{0:T(1024)(128)(4,1)} %bitcast.120), calls=%async_computation.6 | async-start | bytes 4194304
  520.1 35.4 %slice-start.3 = ((s8[10485760]{0:T(1024)(128)(4,1)}), s8[4194304]{0:T(1024)(128)(4,1)S(1)}, s32[]{:S(2)}) async-start(s8[10485760]{0:T(1024)(128)(4,1)} %bitcast.120), calls=%async_computation.7 | async-start | bytes 8388608
  539.1 16.4 %slice-start.4 = ((s8[10485760]{0:T(1024)(128)(4,1)}), s8[4194304]{0:T(1024)(128)(4,1)S(1)}, s32[]{:S(2)}) async-start(s8[10485760]{0:T(1024)(128)(4,1)} %bitcast.120), calls=%async_computation.8 | async-start | bytes 8388608
  575.3 9.7 %copy-start = (f32[16,2,128,256]{3,2,1,0:T(8,128)S(1)}, f32[16,2,128,256]{3,2,1,0:T(8,128)}, u32[]{:S(2)}) copy-start(f32[16,2,128,256]{3,2,1,0:T(8,128)} %fusion.83) | copy-start | bytes 12582916
  592.6 10.7 %slice-start.5 = ((s8[8388608]{0:T(1024)(128)(4,1)}), s8[4194304]{0:T(1024)(128)(4,1)S(1)}, s32[]{:S(2)}) async-start(s8[8388608]{0:T(1024)(128)(4,1)} %bitcast.128), calls=%async_computation.9 | async-start | bytes 8388608
  597.4 5.9 slice-start.6
  663.4 6.5 copy-start.4
  663.4 100.0 %all-to-all-start.3 = ((bf16[16,1024,2,128]{3,2,0,1:T(2,128)(2,1)}), bf16[16,1024,2,128]{3,2,0,1:T(2,128)(2,1)}, u32[]{:S(2)}, u32[]{:S(2)}) async-start(bf16[16,1024,2,128]{3,2,0,1:T(2,128)(2,1)} %copy.24), calls=%async_computation.3 | async-start | bytes 16777216 | tf_op jit(solution)/shard_map/all_to_all | solution.py:70
where the time goes:
time: 827 us; the launch traced here: 818 us
  waiting for transfers between devices  250 us (30%)
  matrix products  209 us (25%)
  other arithmetic  180 us (22%)
  local copies, waits for them, and re-layouts  153 us (19%)
  starting transfers between devices  25.4 us (3%)
    all_to_all x1, waiting for transfers between devices, local_block(): lax.all_to_all(o_heads, 'sp', 1, 2, tiled=True)  93.5 us
    dot_general x4, matrix products, project(): jnp.einsum('bsd,de->bse', x_tok, weight, preferred_element_type=jnp.float32)  91.7 us
    all_to_all x1, waiting for transfers between devices, local_block(): q_heads = lax.all_to_all(q_loc, 'sp', 2, 1, tiled=True)  82.7 us
    sub x6, other arithmetic, causal_attention(): probs = jax.nn.softmax(scores, axis=-1).astype(jnp.bfloat16)  68.6 us
    all_to_all x1, waiting for transfers between devices, local_block(): k_heads = lax.all_to_all(k_loc, 'sp', 2, 1, tiled=True)  61 us
    dot_general x8, matrix products, causal_attention(): jnp.einsum('bhqk,bkhd->bqhd', probs, v_heads[:, :key_end], preferred_elem...  58.3 us
    another operation x1, other arithmetic  52.6 us
    slice x1, local copies, waits for them, and re-layouts, apply_rope(): first = heads_f32[..., :half]  45.6 us
  transfers between devices with their start and end apart: 4, of which 4 were waited for; matrix products, arithmetic and copies ran while one was open for 15% of the time, Pallas kernels for 0%

commit v1 on v0

v1 whole, which is shorter than its diff:
```python
import functools

import numpy as np
import jax
import jax.numpy as jnp
from jax import lax
from jax.experimental import pallas as pl
from jax.experimental.pallas import tpu as pltpu
from jax.sharding import PartitionSpec as P

HEAD_DIM = 128
HALF = HEAD_DIM // 2
ROPE_THETA = 500000.0
NORM_EPS = 1e-6
SCALE = HEAD_DIM ** -0.5
EXP2_SCALE = SCALE * 1.4426950408889634
NEG = -1e30
TN = 512
F32 = jnp.float32
BF16 = jnp.bfloat16


def kernel(n, per, blk, width,
           x_hbm, pos_hbm, wq_hbm, wk_hbm, wv_hbm, wo_hbm, gq_ref, gk_ref, freq_ref,
           xr_hbm, a_hbm,
           wq, wk, wv, wo, q_buf, k_buf, v_buf, x_buf, pos_buf, c_tab, s_tab, r_q, r_k,
           w_sem, own_sem, ld_sem, aloc_sem, x_send, x_recv, p_send, p_recv, a_send, a_recv):
    chips = n // 2
    ch = 2 * blk
    seq = n * blk
    heads = width // HEAD_DIM
    tiles = width // TN
    per_tile = TN // HEAD_DIM
    me = lax.axis_index('sp')
    my_chip = me // 2
    my_core = me % 2
    sib = 2 * my_chip + (1 - my_core)

    weights = [(wq_hbm, wq), (wk_hbm, wk), (wv_hbm, wv), (wo_hbm, wo)]

    def weight_copy(i):
        return pltpu.make_async_copy(weights[i][0], weights[i][1], w_sem.at[i])

    barrier = pltpu.get_barrier_semaphore()
    for d in range(1, n):
        pl.semaphore_signal(barrier, inc=1, device_id={'sp': lax.rem(me + d, n)},
                            device_id_type=pl.DeviceIdType.MESH)
    own_pos = pltpu.make_async_copy(pos_hbm.at[me], pos_buf.at[me], own_sem)
    own_pos.start()
    for i in range(4):
        weight_copy(i).start()
    pl.semaphore_wait(barrier, n - 1)

    partners = [(0, 1)] + [(dc, fl) for dc in ([1, chips - 1] + list(range(2, chips - 1))) for fl in (0, 1)]

    def partner(dc, fl):
        core = my_core if fl == 0 else 1 - my_core
        return 2 * lax.rem(my_chip + dc, chips) + core

    def x_copy(pi, s):
        tgt = partner(*partners[pi])
        return pltpu.make_async_remote_copy(
            src_ref=x_hbm.at[tgt * per + s], dst_ref=xr_hbm.at[s, me],
            send_sem=x_send.at[s, pi], recv_sem=x_recv.at[s, me],
            device_id={'sp': tgt}, device_id_type=pl.DeviceIdType.MESH)

    def pos_copy(pi):
        tgt = partner(*partners[pi])
        return pltpu.make_async_remote_copy(
            src_ref=pos_hbm.at[tgt], dst_ref=pos_buf.at[me],
            send_sem=p_send.at[pi], recv_sem=p_recv.at[me],
            device_id={'sp': tgt}, device_id_type=pl.DeviceIdType.MESH)

    for pi in range(n - 1):
        pos_copy(pi).start()
    for s in range(per):
        for pi in range(n - 1):
            x_copy(pi, s).start()
    own_pos.wait()

    def wait_x(s, src):
        pltpu.make_async_remote_copy(
            src_ref=x_hbm.at[0], dst_ref=xr_hbm.at[s, src], send_sem=x_send.at[s, 0],
            recv_sem=x_recv.at[s, src], device_id={'sp': sib},
            device_id_type=pl.DeviceIdType.MESH).wait_recv()

    def wait_pos(src):
        pltpu.make_async_remote_copy(
            src_ref=pos_hbm.at[0], dst_ref=pos_buf.at[src], send_sem=p_send.at[0],
            recv_sem=p_recv.at[src], device_id={'sp': sib},
            device_id_type=pl.DeviceIdType.MESH).wait_recv()

    def half_copy(src, slot, half):
        return pltpu.make_async_copy(
            src, x_buf.at[slot, pl.ds(pl.multiple_of(half * blk, blk), blk)], ld_sem.at[slot, half])

    def load_own(s, slot):
        half_copy(x_hbm.at[me * per + s], slot, my_core).start()
        wait_x(s, sib)
        half_copy(xr_hbm.at[s, sib], slot, 1 - my_core).start()

    def load_other(s, c, slot):
        for half in range(2):
            wait_x(s, 2 * c + half)
            half_copy(xr_hbm.at[s, 2 * c + half], slot, half).start()

    def wait_load(slot):
        for half in range(2):
            half_copy(xr_hbm.at[0, 0], slot, half).wait()

    n_own = per
    chip_offsets = [1, chips - 1] + list(range(2, chips - 1))

    def offset_of(i):
        out = jnp.int32(chip_offsets[0])
        for j in range(1, len(chip_offsets)):
            out = jnp.where(i == j, jnp.int32(chip_offsets[j]), out)
        return out

    lane = lax.broadcasted_iota(jnp.int32, (blk, HEAD_DIM), 1)
    row = lax.broadcasted_iota(jnp.int32, (blk, HEAD_DIM), 0)

    def tables(s, c):
        for half in range(2):
            p_row = pos_buf[2 * c + half, s, 0:1, :]
            sel = jnp.where(lane == row, jnp.broadcast_to(p_row, (blk, HEAD_DIM)), 0)
            p_col = jnp.sum(sel.astype(F32), axis=1, keepdims=True)
            ang = p_col * freq_ref[...]
            rows = pl.ds(half * blk, blk)
            c_tab[rows, :] = jnp.cos(ang)
            sn = jnp.sin(ang)
            s_tab[rows, :] = jnp.where(lane < HALF, -sn, sn)

    def rope_heads(buf, row0, r_ref, g_ref, j):
        for hh in range(per_tile):
            cols = pl.ds(pl.multiple_of(j * TN + hh * HEAD_DIM, HEAD_DIM), HEAD_DIM)
            u = buf[pl.ds(row0, ch), cols].astype(F32) * r_ref[...] * g_ref[0:1, cols].astype(F32)
            rot = pltpu.roll(u, HALF, 1)
            buf[pl.ds(row0, ch), cols] = (u * c_tab[...] + rot * s_tab[...]).astype(BF16)

    def proj_tile(x, w, dst, row0, j, acc):
        cols = pl.ds(pl.multiple_of(j * TN, TN), TN)
        p = jnp.dot(x[...], w[:, cols], preferred_element_type=F32).astype(BF16)
        dst[pl.ds(row0, ch), cols] = p
        if acc is None:
            return None
        pf = p.astype(F32)
        sq = pf * pf
        for t in range(per_tile):
            acc = acc + sq[:, t * HEAD_DIM:(t + 1) * HEAD_DIM]
        return acc

    def inv_rms(acc):
        ss = jnp.sum(acc, axis=1, keepdims=True)
        return jnp.broadcast_to(lax.rsqrt(ss * (1.0 / width) + NORM_EPS), (ch, HEAD_DIM))

    def qkv_chunk(s, c, slot, first, prefetch):
        row0 = pl.multiple_of(s * seq + c * ch, ch)
        x = x_buf.at[slot]
        wait_load(slot)
        tables(s, c)

        @pl.when(first)
        def _():
            weight_copy(0).wait()

        zero = jnp.zeros((ch, HEAD_DIM), F32)
        acc = lax.fori_loop(0, tiles, lambda j, acc: proj_tile(x, wq, q_buf, row0, j, acc), zero)
        r_q[...] = inv_rms(acc)

        @pl.when(first)
        def _():
            weight_copy(1).wait()

        def k_step(j, acc):
            acc = proj_tile(x, wk, k_buf, row0, j, acc)
            rope_heads(q_buf, row0, r_q, gq_ref, j)
            return acc
        acc = lax.fori_loop(0, tiles, k_step, zero)
        r_k[...] = inv_rms(acc)

        @pl.when(first)
        def _():
            weight_copy(2).wait()

        prefetch()

        def v_step(j, carry):
            proj_tile(x, wv, v_buf, row0, j, None)
            rope_heads(k_buf, row0, r_k, gk_ref, j)
            return carry
        lax.fori_loop(0, tiles, v_step, 0)

    dr = lax.broadcasted_iota(jnp.int32, (ch, ch), 0)
    dc_ = lax.broadcasted_iota(jnp.int32, (ch, ch), 1)
    diag_mask = dc_ <= dr
    nt = (((1,), (1,)), ((), ()))

    def attend(s):
        base = pl.multiple_of(s * seq, seq)

        def head(h, carry):
            cols = pl.ds(pl.multiple_of(h * HEAD_DIM, HEAD_DIM), HEAD_DIM)
            for i in range(chips):
                rows = pl.ds(base + i * ch, ch)
                q = q_buf[rows, cols]
                kd = k_buf[rows, cols]
                sd = lax.dot_general(q, kd, nt, preferred_element_type=F32)
                sd = jnp.where(diag_mask, sd, NEG)
                m = jnp.max(sd, axis=1, keepdims=True)
                if i:
                    past = pl.ds(base, i * ch)
                    sp_ = lax.dot_general(q, k_buf[past, cols], nt, preferred_element_type=F32)
                    m = jnp.maximum(m, jnp.max(sp_, axis=1, keepdims=True))
                ms = m * EXP2_SCALE
                ed = jnp.exp2(sd * EXP2_SCALE - ms)
                l = jnp.sum(ed, axis=1, keepdims=True)
                if i:
                    ep = jnp.exp2(sp_ * EXP2_SCALE - ms)
                    l = l + jnp.sum(ep, axis=1, keepdims=True)
                inv = 1.0 / l
                o = jnp.dot((ed * inv).astype(BF16), v_buf[rows, cols], preferred_element_type=F32)
                if i:
                    o = o + jnp.dot((ep * inv).astype(BF16), v_buf[past, cols], preferred_element_type=F32)
                q_buf[rows, cols] = o.astype(BF16)
            return carry
        lax.fori_loop(0, heads, head, 0)

    def a_rows(s, c, core):
        return k_buf.at[pl.ds(pl.multiple_of(s * seq + c * ch + core * blk, blk), blk)]

    def a_copy(s, c, core):
        tgt = 2 * c + core
        return pltpu.make_async_remote_copy(
            src_ref=a_rows(s, c, core), dst_ref=a_hbm.at[me * per + s],
            send_sem=a_send.at[s, tgt], recv_sem=a_recv.at[s, me],
            device_id={'sp': tgt}, device_id_type=pl.DeviceIdType.MESH)

    def a_local(s):
        return pltpu.make_async_copy(a_rows(s, my_chip, my_core), a_hbm.at[me * per + s], aloc_sem.at[s])

    def out_chunk(s, c):
        row0 = pl.multiple_of(s * seq + c * ch, ch)

        def step(j, carry):
            cols = pl.ds(pl.multiple_of(j * TN, TN), TN)
            k_buf[pl.ds(row0, ch), cols] = jnp.dot(
                q_buf[pl.ds(row0, ch), :], wo[:, cols], preferred_element_type=F32).astype(BF16)
            return carry
        lax.fori_loop(0, tiles, step, 0)

    def phase(s, carry):
        lo = jnp.where(s == 0, 0, n_own)
        start = jnp.where(s == 0, -n_own, 0)

        @pl.when(s == 0)
        def _():
            load_own(0, 0)

        @pl.when(s > 0)
        def _():
            load_other(s, lax.rem(my_chip + offset_of(0), chips), 0)

        def chunk(i, carry):
            own = i < 0
            sq = jnp.where(own, i + n_own, s)
            c = jnp.where(own, my_chip, lax.rem(my_chip + offset_of(i), chips))
            slot = lax.rem(i - start, 2)

            def prefetch():
                nxt = i + 1

                @pl.when(nxt < 0)
                def _():
                    load_own(nxt + n_own, 1 - slot)

                @pl.when(jnp.logical_and(nxt >= 0, nxt < chips - 1))
                def _():
                    load_other(s, lax.rem(my_chip + offset_of(nxt), chips), 1 - slot)

            @pl.when(jnp.logical_and(s == 0, i == -n_own))
            def _():
                for d in range(1, n):
                    wait_pos(lax.rem(me + d, n))
            qkv_chunk(sq, c, slot, jnp.logical_and(s == 0, i == -n_own), prefetch)
            return carry
        lax.fori_loop(start, chips - 1, chunk, 0)

        attend(s)

        @pl.when(s == 0)
        def _():
            weight_copy(3).wait()

        def out_step(i, carry):
            c = jnp.where(i == chips - 1, my_chip, lax.rem(my_chip + offset_of(i), chips))
            out_chunk(s, c)
            for core in range(2):
                mine = jnp.logical_and(c == my_chip, core == my_core)

                @pl.when(mine)
                def _():
                    a_local(s).start()

                @pl.when(jnp.logical_not(mine))
                def _():
                    a_copy(s, c, core).start()
            return carry
        lax.fori_loop(0, chips, out_step, 0)
        return carry

    lax.fori_loop(0, per, phase, 0)

    for s in range(per):
        a_local(s).wait()
        for pi in range(n - 1):
            x_copy(pi, s).wait_send()
            tgt = partner(*partners[pi])
            pltpu.make_async_remote_copy(
                src_ref=k_buf.at[pl.ds(0, blk)], dst_ref=a_hbm.at[tgt * per + s],
                send_sem=a_send.at[s, tgt], recv_sem=a_recv.at[s, tgt],
                device_id={'sp': tgt}, device_id_type=pl.DeviceIdType.MESH).wait()
    for pi in range(n - 1):
        pos_copy(pi).wait_send()


def exchange_attention(n, x_loc, pos_loc, w_query, w_key, w_value, w_out, gain_q, gain_k):
    batch, blk, width = x_loc.shape
    per = batch // n
    seq = n * blk
    freq = (1.0 / (np.float32(ROPE_THETA) ** (np.arange(0, HEAD_DIM, 2, dtype=np.float32) / np.float32(HEAD_DIM)))).astype(np.float32)
    freq = jnp.asarray(np.concatenate([freq, freq])[None, :])
    pos8 = jnp.broadcast_to(pos_loc.reshape(n, per, 1, blk), (n, per, 8, blk))
    hbm = pl.BlockSpec(memory_space=pl.ANY)
    vmem = pl.BlockSpec(memory_space=pltpu.VMEM)
    dma = pltpu.SemaphoreType.DMA
    wbuf = pltpu.VMEM((width, width), BF16)
    sbuf = pltpu.VMEM((per * seq, width), BF16)
    tab = pltpu.VMEM((2 * blk, HEAD_DIM), F32)
    _, a_all = pl.pallas_call(
        functools.partial(kernel, n, per, blk, width),
        out_shape=(jax.ShapeDtypeStruct((per, n, blk, width), BF16), jax.ShapeDtypeStruct((batch, blk, width), BF16)),
        in_specs=[hbm] * 6 + [vmem] * 3,
        out_specs=(hbm, hbm),
        scratch_shapes=[
            wbuf, wbuf, wbuf, wbuf, sbuf, sbuf, sbuf,
            pltpu.VMEM((2, 2 * blk, width), BF16),
            pltpu.VMEM((n, per, 8, blk), jnp.int32),
            tab, tab, tab, tab,
            dma((4,)), dma, dma((2, 2)), dma((per,)),
            dma((per, n)), dma((per, n)), dma((n,)), dma((n,)), dma((per, n)), dma((per, n)),
        ],
        compiler_params=pltpu.CompilerParams(
            collective_id=0, has_side_effects=True, vmem_limit_bytes=67043328),
        name='exchange_attention',
    )(x_loc, pos8, w_query, w_key, w_value, w_out, gain_q.reshape(1, width), gain_k.reshape(1, width), freq)
    return a_all


def solution(mesh):
    n = mesh.shape['sp']

    def local_block(x_loc, pos_loc, w_query, w_key, w_value, w_out, gain_q, gain_k, gain_out):
        a = exchange_attention(n, x_loc, pos_loc, w_query, w_key, w_value, w_out, gain_q, gain_k).astype(F32)
        mean_sq = jnp.mean(a * a, axis=-1, keepdims=True)
        return (x_loc.astype(F32) + a * lax.rsqrt(mean_sq + NORM_EPS) * gain_out.astype(F32)).astype(BF16)

    tok_spec = P('dp', 'sp', None)
    return jax.shard_map(local_block, mesh=mesh, in_specs=(tok_spec, P('dp', 'sp'), P(), P(), P(), P(), P(), P(), P()), out_specs=tok_spec, check_vma=False)
```

time: 827 us -> 270 us (0.33); the launches traced: 818 us -> 269 us
  Pallas kernels: 0 us -> 250 us
  waiting for transfers between devices: 250 us -> 0 us
  matrix products: 209 us -> 0 us
  other arithmetic: 180 us -> 14.5 us
  local copies, waits for them, and re-layouts: 153 us -> 4.41 us
  starting transfers between devices: 25.4 us -> 0 us
    pallas_call x0 -> x1, Pallas kernels: none -> 250 us  [exchange_attention(): pl.pallas_call(functools.partial(kernel, n, per, blk, width), out_shape=(...]
    all_to_all x4 -> x0, waiting for transfers between devices: 250 us -> none  [the longest x1 93.5 us: local_block(): lax.all_to_all(o_heads, 'sp', 1, 2, tiled=True)]
    dot_general x19 -> x0, matrix products: 194 us -> none  [the longest x4 91.7 us: project(): jnp.einsum('bsd,de->bse', x_tok, weight, preferred_element_type=jnp.float32)]
    sub x6 -> x0, other arithmetic: 68.6 us -> none  [causal_attention(): probs = jax.nn.softmax(scores, axis=-1).astype(jnp.bfloat16)]
    another operation x1 -> x0, other arithmetic: 52.6 us -> none
    slice x1 -> x0, local copies, waits for them, and re-layouts: 45.6 us -> none  [apply_rope(): first = heads_f32[..., :half]]
    all_to_all x4 -> x0, local copies, waits for them, and re-layouts: 39.5 us -> none  [the longest x1 10.5 us: local_block(): v_heads = lax.all_to_all(v_loc, 'sp', 2, 1, tiled=True)]
    unnamed x32 -> x4, local copies, waits for them, and re-layouts: 28.5 us -> 0.51 us
  transfers between devices with their start and end apart: 4 -> 0, of which waited for: 4 -> 0; matrix products, arithmetic and copies ran while one was open for 15% -> 0% of each run, Pallas kernels for 0% -> 0%
where the time goes in v1:
time: 270 us; the launch traced here: 269 us
  Pallas kernels  250 us (93%)
  other arithmetic  14.5 us (5%)
  local copies, waits for them, and re-layouts  4.41 us (2%)
    pallas_call x1, Pallas kernels, exchange_attention(): pl.pallas_call(functools.partial(kernel, n, per, blk, width), out_shape=(...  250 us
    convert_element_type x1, other arithmetic, local_block(): (x_loc.astype(F32) + a * lax.rsqrt(mean_sq + NORM_EPS) * gain_out.astype(...  9.23 us

profile of v1, /device:TPU:81, one launch (start us, length us, event | category | flops | bytes accessed | tf_op | source)
XLA Modules:
  0.0 269.3 jit_solution(17279431245524321579)
XLA Ops:
  0.0 1.3 broadcast_in_dim.10.pos_hbm
  1.3 1.3 reshape.17.gq_ref
  2.6 1.3 reshape.18.gk_ref
  3.9 250.3 %exchange_attention.1 = (bf16[2,8,128,2048]{3,2,1,0:T(8,128)(2,1)}, bf16[16,128,2048]{2,1,0:T(8,128)(2,1)}) custom-call(bf16[16,128,2048]{2,1,0:T(8,128)(2,1)} %x_hbm.1, s32[8,2,8,128]{3,2,1,0:T(8,128)} %broadcast_in_dim.10.pos_hbm, bf16[2048,2048]{1,0:T(8,128)(2,1)} %wq_hbm.1, bf16[2048,2048]{1,0:T(8,128)(2,1)} %wk_hbm.1, bf16[2048,2048]{1,0:T(8,128)(2,1)} %wv_hbm.1, ...), custom_call_target="tpu_custom_call" | custom-call | tf_op jit(solution)/shard_map/exchange_attention/pallas_call | solution.py:340
  254.3 0.0 copy-start.1
  254.3 0.0 copy-start
  254.3 5.2 %fusion = f32[16,128]{1,0:T(8,128)S(1)} fusion(bf16[16,128,2048]{2,1,0:T(8,128)(2,1)} %get-tuple-element.6), kind=kLoop, calls=%fused_computation.2 | loop fusion | flops 12580864 | bytes 8396800 | tf_op jit(solution)/shard_map/reduce_sum | solution.py:365
  259.5 0.0 copy-done.1
  259.6 0.5 copy-done
  260.1 9.2 %fusion.3 = bf16[16,128,2048]{2,1,0:T(8,128)(2,1)} fusion(bf16[16,128,2048]{2,1,0:T(8,128)(2,1)} %get-tuple-element.6, bf16[16,128,2048]{2,1,0:T(8,128)(2,1)S(1)} %copy-done, f32[2048]{0:T(1024)S(1)} %convert_element_type.14, f32[16,128]{1,0:T(8,128)S(1)} %add_rsqrt_fusion), kind=kLoop, calls=%fused_computation.5 | loop fusion | flops 25165824 | bytes 25182208 | tf_op jit(solution)/shard_map/convert_element_type | solution.py:366
  (2 shorter events, 0.0 us)
Async XLA Ops:
  254.3 5.3 %copy-start.1 = (bf16[2048]{0:T(1024)(128)(2,1)S(1)}, bf16[2048]{0:T(1024)(128)(2,1)}, u32[]{:S(2)}) copy-start(bf16[2048]{0:T(1024)(128)(2,1)} %param.18) | copy-start | bytes 12292
  254.3 5.8 %copy-start = (bf16[16,128,2048]{2,1,0:T(8,128)(2,1)S(1)}, bf16[16,128,2048]{2,1,0:T(8,128)(2,1)}, u32[]{:S(2)}) copy-start(bf16[16,128,2048]{2,1,0:T(8,128)(2,1)} %x_hbm.1) | copy-start | bytes 25165828

commit v2 on v1

--- a/solution.py
+++ b/solution.py
@@ -21,10 +21,10 @@
 
 
 def kernel(n, per, blk, width,
-           x_hbm, pos_hbm, wq_hbm, wk_hbm, wv_hbm, wo_hbm, gq_ref, gk_ref, freq_ref,
-           xr_hbm, a_hbm,
-           wq, wk, wv, wo, q_buf, k_buf, v_buf, x_buf, pos_buf, c_tab, s_tab, r_q, r_k,
-           w_sem, own_sem, ld_sem, aloc_sem, x_send, x_recv, p_send, p_recv, a_send, a_recv):
+           x_hbm, pos_hbm, wq_hbm, wk_hbm, wv_hbm, wo_hbm, gq_ref, gk_ref, ga_ref, freq_ref,
+           xr_hbm, a_hbm, y_hbm,
+           wq, wk, wv, wo, q_buf, k_buf, vt_buf, x_buf, pos_buf, c_tab, s_tab, r_q, r_k, sc_buf, g_tab,
+           w_sem, own_sem, ld_sem, aloc_sem, out_sem, x_send, x_recv, p_send, p_recv, a_send, a_recv):
     chips = n // 2
     ch = 2 * blk
     seq = n * blk
@@ -45,7 +45,7 @@
     for d in range(1, n):
         pl.semaphore_signal(barrier, inc=1, device_id={'sp': lax.rem(me + d, n)},
                             device_id_type=pl.DeviceIdType.MESH)
-    own_pos = pltpu.make_async_copy(pos_hbm.at[me], pos_buf.at[me], own_sem)
+    own_pos = pltpu.make_async_copy(pos_hbm, pos_buf.at[me], own_sem)
     own_pos.start()
     for i in range(4):
         weight_copy(i).start()
@@ -67,7 +67,7 @@
     def pos_copy(pi):
         tgt = partner(*partners[pi])
         return pltpu.make_async_remote_copy(
-            src_ref=pos_hbm.at[tgt], dst_ref=pos_buf.at[me],
+            src_ref=pos_hbm, dst_ref=pos_buf.at[me],
             send_sem=p_send.at[pi], recv_sem=p_recv.at[me],
             device_id={'sp': tgt}, device_id_type=pl.DeviceIdType.MESH)
 
@@ -77,6 +77,8 @@
         for pi in range(n - 1):
             x_copy(pi, s).start()
     own_pos.wait()
+    for gi, g in enumerate((gq_ref, gk_ref, ga_ref)):
+        g_tab[gi:gi + 1, :] = g[...].astype(F32).reshape(1, width)
 
     def wait_x(s, src):
         pltpu.make_async_remote_copy(
@@ -86,7 +88,7 @@
 
     def wait_pos(src):
         pltpu.make_async_remote_copy(
-            src_ref=pos_hbm.at[0], dst_ref=pos_buf.at[src], send_sem=p_send.at[0],
+            src_ref=pos_hbm, dst_ref=pos_buf.at[src], send_sem=p_send.at[0],
             recv_sem=p_recv.at[src], device_id={'sp': sib},
             device_id_type=pl.DeviceIdType.MESH).wait_recv()
 
@@ -122,7 +124,7 @@
 
     def tables(s, c):
         for half in range(2):
-            p_row = pos_buf[2 * c + half, s, 0:1, :]
+            p_row = pos_buf[2 * c + half, pl.ds(me * per + s, 1), :]
             sel = jnp.where(lane == row, jnp.broadcast_to(p_row, (blk, HEAD_DIM)), 0)
             p_col = jnp.sum(sel.astype(F32), axis=1, keepdims=True)
             ang = p_col * freq_ref[...]
@@ -131,19 +133,17 @@
             sn = jnp.sin(ang)
             s_tab[rows, :] = jnp.where(lane < HALF, -sn, sn)
 
-    def rope_heads(buf, row0, r_ref, g_ref, j):
+    def rope_heads(buf, row0, r_ref, gi, j):
         for hh in range(per_tile):
-            cols = pl.ds(pl.multiple_of(j * TN + hh * HEAD_DIM, HEAD_DIM), HEAD_DIM)
-            u = buf[pl.ds(row0, ch), cols].astype(F32) * r_ref[...] * g_ref[0:1, cols].astype(F32)
+            cols = pl.ds(j * TN + hh * HEAD_DIM, HEAD_DIM)
+            u = buf[pl.ds(row0, ch), cols].astype(F32) * r_ref[...] * g_tab[gi:gi + 1, cols]
             rot = pltpu.roll(u, HALF, 1)
             buf[pl.ds(row0, ch), cols] = (u * c_tab[...] + rot * s_tab[...]).astype(BF16)
 
     def proj_tile(x, w, dst, row0, j, acc):
-        cols = pl.ds(pl.multiple_of(j * TN, TN), TN)
+        cols = pl.ds(j * TN, TN)
         p = jnp.dot(x[...], w[:, cols], preferred_element_type=F32).astype(BF16)
         dst[pl.ds(row0, ch), cols] = p
-        if acc is None:
-            return None
         pf = p.astype(F32)
         sq = pf * pf
         for t in range(per_tile):
@@ -165,18 +165,19 @@
             weight_copy(0).wait()
 
         zero = jnp.zeros((ch, HEAD_DIM), F32)
-        acc = lax.fori_loop(0, tiles, lambda j, acc: proj_tile(x, wq, q_buf, row0, j, acc), zero)
+        acc = zero
+        for j in range(tiles):
+            acc = proj_tile(x, wq, q_buf, row0, j, acc)
         r_q[...] = inv_rms(acc)
 
         @pl.when(first)
         def _():
             weight_copy(1).wait()
 
-        def k_step(j, acc):
+        acc = zero
+        for j in range(tiles):
             acc = proj_tile(x, wk, k_buf, row0, j, acc)
-            rope_heads(q_buf, row0, r_q, gq_ref, j)
-            return acc
-        acc = lax.fori_loop(0, tiles, k_step, zero)
+            rope_heads(q_buf, row0, r_q, 0, j)
         r_k[...] = inv_rms(acc)
 
         @pl.when(first)
@@ -185,44 +186,56 @@
 
         prefetch()
 
-        def v_step(j, carry):
-            proj_tile(x, wv, v_buf, row0, j, None)
-            rope_heads(k_buf, row0, r_k, gk_ref, j)
-            return carry
-        lax.fori_loop(0, tiles, v_step, 0)
+        for j in range(tiles):
+            cols = pl.ds(j * TN, TN)
+            v = jnp.dot(x[...], wv[:, cols], preferred_element_type=F32)
+            vt_buf[s, cols, pl.ds(pl.multiple_of(c * ch, ch), ch)] = v.T.astype(BF16)
+            rope_heads(k_buf, row0, r_k, 1, j)
 
     dr = lax.broadcasted_iota(jnp.int32, (ch, ch), 0)
     dc_ = lax.broadcasted_iota(jnp.int32, (ch, ch), 1)
-    diag_mask = dc_ <= dr
+    diag_mask = dr <= dc_
     nt = (((1,), (1,)), ((), ()))
 
+    groups = [(g, chips - 1 - g) for g in range(chips // 2)]
+
+    def scores(s, h, gi):
+        base = pl.multiple_of(s * seq, seq)
+        cols = pl.ds(pl.multiple_of(h * HEAD_DIM, HEAD_DIM), HEAD_DIM)
+        off = 0
+        for i in groups[gi]:
+            rows = pl.ds(base + i * ch, ch)
+            q = q_buf[rows, cols]
+            if i:
+                sc_buf[gi % 2, off:off + i * ch, :] = lax.dot_general(
+                    k_buf[pl.ds(base, i * ch), cols], q, nt, preferred_element_type=F32)
+            sd = lax.dot_general(k_buf[rows, cols], q, nt, preferred_element_type=F32)
+            sc_buf[gi % 2, off + i * ch:off + (i + 1) * ch, :] = jnp.where(diag_mask, sd, NEG)
+            off += (i + 1) * ch
+
+    def weigh(s, h, gi):
+        base = pl.multiple_of(s * seq, seq)
+        cols = pl.ds(pl.multiple_of(h * HEAD_DIM, HEAD_DIM), HEAD_DIM)
+        off = 0
+        for i in groups[gi]:
+            sc = sc_buf[gi % 2, off:off + (i + 1) * ch, :]
+            m = jnp.max(sc, axis=0, keepdims=True) * EXP2_SCALE
+            e = jnp.exp2(sc * EXP2_SCALE - m)
+            inv = 1.0 / jnp.sum(e, axis=0, keepdims=True)
+            o = jnp.dot(vt_buf[s, cols, 0:(i + 1) * ch], (e * inv).astype(BF16), preferred_element_type=F32)
+            q_buf[pl.ds(base + i * ch, ch), cols] = o.T.astype(BF16)
+            off += (i + 1) * ch
+
     def attend(s):
-        base = pl.multiple_of(s * seq, seq)
+        scores(s, 0, 0)
 
         def head(h, carry):
-            cols = pl.ds(pl.multiple_of(h * HEAD_DIM, HEAD_DIM), HEAD_DIM)
-            for i in range(chips):
-                rows = pl.ds(base + i * ch, ch)
-                q = q_buf[rows, cols]
-                kd = k_buf[rows, cols]
-                sd = lax.dot_general(q, kd, nt, preferred_element_type=F32)
-                sd = jnp.where(diag_mask, sd, NEG)
-                m = jnp.max(sd, axis=1, keepdims=True)
-                if i:
-                    past = pl.ds(base, i * ch)
-                    sp_ = lax.dot_general(q, k_buf[past, cols], nt, preferred_element_type=F32)
-                    m = jnp.maximum(m, jnp.max(sp_, axis=1, keepdims=True))
-                ms = m * EXP2_SCALE
-                ed = jnp.exp2(sd * EXP2_SCALE - ms)
-                l = jnp.sum(ed, axis=1, keepdims=True)
-                if i:
-                    ep = jnp.exp2(sp_ * EXP2_SCALE - ms)
-                    l = l + jnp.sum(ep, axis=1, keepdims=True)
-                inv = 1.0 / l
-                o = jnp.dot((ed * inv).astype(BF16), v_buf[rows, cols], preferred_element_type=F32)
-                if i:
-                    o = o + jnp.dot((ep * inv).astype(BF16), v_buf[past, cols], preferred_element_type=F32)
-                q_buf[rows, cols] = o.astype(BF16)
+            for gi in range(len(groups)):
+                if gi + 1 < len(groups):
+                    scores(s, h, gi + 1)
+                else:
+                    scores(s, lax.rem(h + 1, heads), 0)
+                weigh(s, h, gi)
             return carry
         lax.fori_loop(0, heads, head, 0)
 
@@ -242,12 +255,10 @@
     def out_chunk(s, c):
         row0 = pl.multiple_of(s * seq + c * ch, ch)
 
-        def step(j, carry):
-            cols = pl.ds(pl.multiple_of(j * TN, TN), TN)
+        for j in range(tiles):
+            cols = pl.ds(j * TN, TN)
             k_buf[pl.ds(row0, ch), cols] = jnp.dot(
                 q_buf[pl.ds(row0, ch), :], wo[:, cols], preferred_element_type=F32).astype(BF16)
-            return carry
-        lax.fori_loop(0, tiles, step, 0)
 
     def phase(s, carry):
         lo = jnp.where(s == 0, 0, n_own)
@@ -311,59 +322,114 @@
 
     lax.fori_loop(0, per, phase, 0)
 
+    def a_arrival(s, src):
+        return pltpu.make_async_remote_copy(
+            src_ref=k_buf.at[pl.ds(0, blk)], dst_ref=a_hbm.at[src * per + s],
+            send_sem=a_send.at[s, src], recv_sem=a_recv.at[s, src],
+            device_id={'sp': sib}, device_id_type=pl.DeviceIdType.MESH)
+
+    def source(t):
+        s = t // n
+        r = lax.rem(t, n)
+        return s, lax.rem(me + r, n)
+
+    def fin_loads(t, slot):
+        s, src = source(t)
+        return (pltpu.make_async_copy(a_hbm.at[src * per + s], x_buf.at[slot, pl.ds(0, blk)], ld_sem.at[slot, 0]),
+                pltpu.make_async_copy(x_hbm.at[src * per + s], x_buf.at[slot, pl.ds(blk, blk)], ld_sem.at[slot, 1]))
+
+    def fin_store(t, slot):
+        s, src = source(t)
+        return pltpu.make_async_copy(x_buf.at[slot, pl.ds(0, blk)], y_hbm.at[src * per + s], out_sem.at[slot])
+
+    def fin_fetch(t, slot):
+        s, src = source(t)
+
+        @pl.when(src == me)
+        def _():
+            a_local(s).wait()
+
+        @pl.when(src != me)
+        def _():
+            a_arrival(s, src).wait_recv()
+        for cp in fin_loads(t, slot):
+            cp.start()
+
+    steps = per * n
+    fin_fetch(0, 0)
+
+    def fin_step(t, carry):
+        slot = lax.rem(t, 2)
+
+        @pl.when(t >= 1)
+        def _():
+            fin_store(t - 1, 1 - slot).wait()
+
+        @pl.when(t + 1 < steps)
+        def _():
+            fin_fetch(t + 1, 1 - slot)
+        for cp in fin_loads(t, slot):
+            cp.wait()
+        acc = jnp.zeros((blk, HEAD_DIM), F32)
+        for h in range(heads):
+            v = x_buf[slot, 0:blk, h * HEAD_DIM:(h + 1) * HEAD_DIM].astype(F32)
+            acc = acc + v * v
+        r = lax.rsqrt(jnp.sum(acc, axis=1, keepdims=True) * (1.0 / width) + NORM_EPS)
+        for h in range(heads):
+            cols = slice(h * HEAD_DIM, (h + 1) * HEAD_DIM)
+            v = x_buf[slot, 0:blk, cols].astype(F32) * r * g_tab[2:3, cols]
+            x_buf[slot, 0:blk, cols] = (x_buf[slot, blk:2 * blk, cols].astype(F32) + v).astype(BF16)
+        fin_store(t, slot).start()
+        return carry
+    lax.fori_loop(0, steps, fin_step, 0)
+    fin_store(steps - 1, (steps - 1) % 2).wait()
+
     for s in range(per):
-        a_local(s).wait()
         for pi in range(n - 1):
             x_copy(pi, s).wait_send()
-            tgt = partner(*partners[pi])
-            pltpu.make_async_remote_copy(
-                src_ref=k_buf.at[pl.ds(0, blk)], dst_ref=a_hbm.at[tgt * per + s],
-                send_sem=a_send.at[s, tgt], recv_sem=a_recv.at[s, tgt],
-                device_id={'sp': tgt}, device_id_type=pl.DeviceIdType.MESH).wait()
+            a_arrival(s, partner(*partners[pi])).wait_send()
     for pi in range(n - 1):
         pos_copy(pi).wait_send()
 
 
-def exchange_attention(n, x_loc, pos_loc, w_query, w_key, w_value, w_out, gain_q, gain_k):
+def exchange_attention(n, x_loc, pos_loc, w_query, w_key, w_value, w_out, gain_q, gain_k, gain_out):
     batch, blk, width = x_loc.shape
     per = batch // n
     seq = n * blk
     freq = (1.0 / (np.float32(ROPE_THETA) ** (np.arange(0, HEAD_DIM, 2, dtype=np.float32) / np.float32(HEAD_DIM)))).astype(np.float32)
     freq = jnp.asarray(np.concatenate([freq, freq])[None, :])
-    pos8 = jnp.broadcast_to(pos_loc.reshape(n, per, 1, blk), (n, per, 8, blk))
     hbm = pl.BlockSpec(memory_space=pl.ANY)
     vmem = pl.BlockSpec(memory_space=pltpu.VMEM)
     dma = pltpu.SemaphoreType.DMA
     wbuf = pltpu.VMEM((width, width), BF16)
     sbuf = pltpu.VMEM((per * seq, width), BF16)
     tab = pltpu.VMEM((2 * blk, HEAD_DIM), F32)
-    _, a_all = pl.pallas_call(
+    return pl.pallas_call(
         functools.partial(kernel, n, per, blk, width),
-        out_shape=(jax.ShapeDtypeStruct((per, n, blk, width), BF16), jax.ShapeDtypeStruct((batch, blk, width), BF16)),
-        in_specs=[hbm] * 6 + [vmem] * 3,
-        out_specs=(hbm, hbm),
+        out_shape=(jax.ShapeDtypeStruct((per, n, blk, width), BF16), jax.ShapeDtypeStruct((batch, blk, width), BF16),
+                   jax.ShapeDtypeStruct((batch, blk, width), BF16)),
+        in_specs=[hbm] * 6 + [vmem] * 4,
+        out_specs=(hbm, hbm, hbm),
         scratch_shapes=[
-            wbuf, wbuf, wbuf, wbuf, sbuf, sbuf, sbuf,
+            wbuf, wbuf, wbuf, wbuf, sbuf, sbuf, pltpu.VMEM((per, width, seq), BF16),
             pltpu.VMEM((2, 2 * blk, width), BF16),
-            pltpu.VMEM((n, per, 8, blk), jnp.int32),
+            pltpu.VMEM((n, batch, blk), jnp.int32),
             tab, tab, tab, tab,
-            dma((4,)), dma, dma((2, 2)), dma((per,)),
+            pltpu.VMEM((2, seq + 2 * blk, 2 * blk), F32), pltpu.VMEM((3, width), F32),
+            dma((4,)), dma, dma((2, 2)), dma((per,)), dma((2,)),
             dma((per, n)), dma((per, n)), dma((n,)), dma((n,)), dma((per, n)), dma((per, n)),
         ],
         compiler_params=pltpu.CompilerParams(
             collective_id=0, has_side_effects=True, vmem_limit_bytes=67043328),
         name='exchange_attention',
-    )(x_loc, pos8, w_query, w_key, w_value, w_out, gain_q.reshape(1, width), gain_k.reshape(1, width), freq)
-    return a_all
+    )(x_loc, pos_loc, w_query, w_key, w_value, w_out, gain_q, gain_k, gain_out, freq)[2]
 
 
 def solution(mesh):
     n = mesh.shape['sp']
 
     def local_block(x_loc, pos_loc, w_query, w_key, w_value, w_out, gain_q, gain_k, gain_out):
-        a = exchange_attention(n, x_loc, pos_loc, w_query, w_key, w_value, w_out, gain_q, gain_k).astype(F32)
-        mean_sq = jnp.mean(a * a, axis=-1, keepdims=True)
-        return (x_loc.astype(F32) + a * lax.rsqrt(mean_sq + NORM_EPS) * gain_out.astype(F32)).astype(BF16)
+        return exchange_attention(n, x_loc, pos_loc, w_query, w_key, w_value, w_out, gain_q, gain_k, gain_out)
 
     tok_spec = P('dp', 'sp', None)
     return jax.shard_map(local_block, mesh=mesh, in_specs=(tok_spec, P('dp', 'sp'), P(), P(), P(), P(), P(), P(), P()), out_specs=tok_spec, check_vma=False)

time: 270 us -> 213 us (0.79)
  Pallas kernels: 250 us -> 204 us
  other arithmetic: 14.5 us -> 0 us
  local copies, waits for them, and re-layouts: 4.41 us -> 8.44 us
    pallas_call x1, Pallas kernels: 250 us -> 204 us  [exchange_attention(): pl.pallas_call(functools.partial(kernel, n, per, blk, width), out_shape=(...]
    convert_element_type x2 -> x0, other arithmetic: 9.24 us -> none  [the longest x1 9.23 us: local_block(): (x_loc.astype(F32) + a * lax.rsqrt(mean_sq + NORM_EPS) * gain_out.astype(...]
    unnamed x4 -> x1, local copies, waits for them, and re-layouts: 0.51 us -> 8.44 us
    reduce_sum x1 -> x0, other arithmetic: 5.23 us -> none  [local_block(): mean_sq = jnp.mean(a * a, axis=-1, keepdims=True)]
where the time goes in v2:
time: 213 us
  Pallas kernels  204 us (96%)
  local copies, waits for them, and re-layouts  8.44 us (4%)
    pallas_call x1, Pallas kernels, exchange_attention(): pl.pallas_call(functools.partial(kernel, n, per, blk, width), out_shape=(...  204 us
    unnamed x1, local copies, waits for them, and re-layouts  8.44 us

profile of v2, /device:TPU:81, one launch (start us, length us, event | category | flops | bytes accessed | tf_op | source)
XLA Modules:
  0.0 212.6 jit_solution(8967252313929668044)
XLA Ops:
  0.0 204.2 %exchange_attention.1 = (bf16[2,8,128,2048]{3,2,1,0:T(8,128)(2,1)}, bf16[16,128,2048]{2,1,0:T(8,128)(2,1)}, bf16[16,128,2048]{2,1,0:T(8,128)(2,1)}) custom-call(bf16[16,128,2048]{2,1,0:T(8,128)(2,1)} %x_hbm.1, s32[16,128]{1,0:T(8,128)} %pos_hbm.1, bf16[2048,2048]{1,0:T(8,128)(2,1)} %wq_hbm.1, bf16[2048,2048]{1,0:T(8,128)(2,1)} %wk_hbm.1, ...), custom_call_target="tpu_custom_call" | custom-call | tf_op jit(solution)/shard_map/exchange_attention/pallas_call | solution.py:407
  204.2 8.4 %copy.12 = bf16[16,128,2048]{2,1,0:T(8,128)(2,1)} copy(bf16[16,128,2048]{2,1,0:T(8,128)(2,1)} %get-tuple-element.6) | data formatting | bytes 16777216

commit v3 on v2

--- a/solution.py
+++ b/solution.py
@@ -16,6 +16,7 @@
 EXP2_SCALE = SCALE * 1.4426950408889634
 NEG = -1e30
 TN = 512
+UNROLL = 4
 F32 = jnp.float32
 BF16 = jnp.bfloat16
 
@@ -23,7 +24,7 @@
 def kernel(n, per, blk, width,
            x_hbm, pos_hbm, wq_hbm, wk_hbm, wv_hbm, wo_hbm, gq_ref, gk_ref, ga_ref, freq_ref,
            xr_hbm, a_hbm, y_hbm,
-           wq, wk, wv, wo, q_buf, k_buf, vt_buf, x_buf, pos_buf, c_tab, s_tab, r_q, r_k, sc_buf, g_tab,
+           wq, wk, wv, wo, q_buf, k_buf, vt_buf, x_buf, pos_buf, c_tab, s_tab, r_q, r_k, sc_buf, o_buf, g_tab,
            w_sem, own_sem, ld_sem, aloc_sem, out_sem, x_send, x_recv, p_send, p_recv, a_send, a_recv):
     chips = n // 2
     ch = 2 * blk
@@ -197,50 +198,39 @@
     diag_mask = dr <= dc_
     nt = (((1,), (1,)), ((), ()))
 
-    groups = [(g, chips - 1 - g) for g in range(chips // 2)]
-
-    def scores(s, h, gi):
+    def scores(s, i, h, slot):
         base = pl.multiple_of(s * seq, seq)
         cols = pl.ds(pl.multiple_of(h * HEAD_DIM, HEAD_DIM), HEAD_DIM)
-        off = 0
-        for i in groups[gi]:
-            rows = pl.ds(base + i * ch, ch)
-            q = q_buf[rows, cols]
-            if i:
-                sc_buf[gi % 2, off:off + i * ch, :] = lax.dot_general(
-                    k_buf[pl.ds(base, i * ch), cols], q, nt, preferred_element_type=F32)
-            sd = lax.dot_general(k_buf[rows, cols], q, nt, preferred_element_type=F32)
-            sc_buf[gi % 2, off + i * ch:off + (i + 1) * ch, :] = jnp.where(diag_mask, sd, NEG)
-            off += (i + 1) * ch
-
-    def weigh(s, h, gi):
+        rows = pl.ds(base + i * ch, ch)
+        q = q_buf[rows, cols]
+        if i:
+            sc_buf[slot, 0:i * ch, :] = lax.dot_general(
+                k_buf[pl.ds(base, i * ch), cols], q, nt, preferred_element_type=F32)
+        sd = lax.dot_general(k_buf[rows, cols], q, nt, preferred_element_type=F32)
+        sc_buf[slot, i * ch:(i + 1) * ch, :] = jnp.where(diag_mask, sd, NEG)
+
+    def weigh(s, i, h, slot):
         base = pl.multiple_of(s * seq, seq)
         cols = pl.ds(pl.multiple_of(h * HEAD_DIM, HEAD_DIM), HEAD_DIM)
-        off = 0
-        for i in groups[gi]:
-            sc = sc_buf[gi % 2, off:off + (i + 1) * ch, :]
-            m = jnp.max(sc, axis=0, keepdims=True) * EXP2_SCALE
-            e = jnp.exp2(sc * EXP2_SCALE - m)
-            inv = 1.0 / jnp.sum(e, axis=0, keepdims=True)
-            o = jnp.dot(vt_buf[s, cols, 0:(i + 1) * ch], (e * inv).astype(BF16), preferred_element_type=F32)
-            q_buf[pl.ds(base + i * ch, ch), cols] = o.T.astype(BF16)
-            off += (i + 1) * ch
-
-    def attend(s):
-        scores(s, 0, 0)
-
-        def head(h, carry):
-            for gi in range(len(groups)):
-                if gi + 1 < len(groups):
-                    scores(s, h, gi + 1)
-                else:
-                    scores(s, lax.rem(h + 1, heads), 0)
-                weigh(s, h, gi)
+        sc = sc_buf[slot, 0:(i + 1) * ch, :]
+        m = jnp.max(sc, axis=0, keepdims=True) * EXP2_SCALE
+        e = jnp.exp2(sc * EXP2_SCALE - m)
+        inv = 1.0 / jnp.sum(e, axis=0, keepdims=True)
+        o = jnp.dot(vt_buf[s, cols, 0:(i + 1) * ch], (e * inv).astype(BF16), preferred_element_type=F32)
+        o_buf[:, cols] = o.T.astype(BF16)
+
+    def attend(s, i):
+        scores(s, i, 0, 0)
+
+        def some(g, carry):
+            for u in range(UNROLL):
+                scores(s, i, lax.rem(UNROLL * g + u + 1, heads), (u + 1) % 2)
+                weigh(s, i, UNROLL * g + u, u % 2)
             return carry
-        lax.fori_loop(0, heads, head, 0)
+        lax.fori_loop(0, heads // UNROLL, some, 0)
 
     def a_rows(s, c, core):
-        return k_buf.at[pl.ds(pl.multiple_of(s * seq + c * ch + core * blk, blk), blk)]
+        return q_buf.at[pl.ds(pl.multiple_of(s * seq + c * ch + core * blk, blk), blk)]
 
     def a_copy(s, c, core):
         tgt = 2 * c + core
@@ -257,8 +247,8 @@
 
         for j in range(tiles):
             cols = pl.ds(j * TN, TN)
-            k_buf[pl.ds(row0, ch), cols] = jnp.dot(
-                q_buf[pl.ds(row0, ch), :], wo[:, cols], preferred_element_type=F32).astype(BF16)
+            q_buf[pl.ds(row0, ch), cols] = jnp.dot(
+                o_buf[...], wo[:, cols], preferred_element_type=F32).astype(BF16)
 
     def phase(s, carry):
         lo = jnp.where(s == 0, 0, n_own)
@@ -297,14 +287,16 @@
             return carry
         lax.fori_loop(start, chips - 1, chunk, 0)
 
-        attend(s)
-
         @pl.when(s == 0)
         def _():
             weight_copy(3).wait()
 
         def out_step(i, carry):
             c = jnp.where(i == chips - 1, my_chip, lax.rem(my_chip + offset_of(i), chips))
+            for blk_i in range(chips):
+                @pl.when(c == blk_i)
+                def _():
+                    attend(s, blk_i)
             out_chunk(s, c)
             for core in range(2):
                 mine = jnp.logical_and(c == my_chip, core == my_core)
@@ -322,16 +314,21 @@
 
     lax.fori_loop(0, per, phase, 0)
 
+    home = [(0, 1)] + [(dc, fl) for fl in (0, 1) for dc in (chips - 1, 1)] + partners[5:]
+
     def a_arrival(s, src):
         return pltpu.make_async_remote_copy(
-            src_ref=k_buf.at[pl.ds(0, blk)], dst_ref=a_hbm.at[src * per + s],
+            src_ref=q_buf.at[pl.ds(0, blk)], dst_ref=a_hbm.at[src * per + s],
             send_sem=a_send.at[s, src], recv_sem=a_recv.at[s, src],
             device_id={'sp': sib}, device_id_type=pl.DeviceIdType.MESH)
 
     def source(t):
         s = t // n
         r = lax.rem(t, n)
-        return s, lax.rem(me + r, n)
+        src = me
+        for k, (dc, fl) in enumerate(home):
+            src = jnp.where(r == k + 1, partner(dc, fl), src)
+        return s, src
 
     def fin_loads(t, slot):
         s, src = source(t)
@@ -415,7 +412,7 @@
             pltpu.VMEM((2, 2 * blk, width), BF16),
             pltpu.VMEM((n, batch, blk), jnp.int32),
             tab, tab, tab, tab,
-            pltpu.VMEM((2, seq + 2 * blk, 2 * blk), F32), pltpu.VMEM((3, width), F32),
+            pltpu.VMEM((2, seq, 2 * blk), F32), pltpu.VMEM((2 * blk, width), BF16), pltpu.VMEM((3, width), F32),
             dma((4,)), dma, dma((2, 2)), dma((per,)), dma((2,)),
             dma((per, n)), dma((per, n)), dma((n,)), dma((n,)), dma((per, n)), dma((per, n)),
         ],

time: 213 us -> 205 us (0.962)
  the two profiles are of different devices: /device:TPU:81 before, /device:TPU:83 now
where the time goes in v3:
time: 205 us; the launch traced here: 204 us
  Pallas kernels  196 us (96%)
  local copies, waits for them, and re-layouts  8.44 us (4%)
    pallas_call x1, Pallas kernels, exchange_attention(): pl.pallas_call(functools.partial(kernel, n, per, blk, width), out_shape=(...  196 us
    unnamed x1, local copies, waits for them, and re-layouts  8.44 us

profile of v3, /device:TPU:83, one launch (start us, length us, event | category | flops | bytes accessed | tf_op | source)
XLA Modules:
  0.0 204.5 jit_solution(7733161168583209393)
XLA Ops:
  0.0 196.0 %exchange_attention.1 = (bf16[2,8,128,2048]{3,2,1,0:T(8,128)(2,1)}, bf16[16,128,2048]{2,1,0:T(8,128)(2,1)}, bf16[16,128,2048]{2,1,0:T(8,128)(2,1)}) custom-call(bf16[16,128,2048]{2,1,0:T(8,128)(2,1)} %x_hbm.1, s32[16,128]{1,0:T(8,128)} %pos_hbm.1, bf16[2048,2048]{1,0:T(8,128)(2,1)} %wq_hbm.1, bf16[2048,2048]{1,0:T(8,128)(2,1)} %wk_hbm.1, ...), custom_call_target="tpu_custom_call" | custom-call | tf_op jit(solution)/shard_map/exchange_attention/pallas_call | solution.py:404
  196.0 8.4 %copy.12 = bf16[16,128,2048]{2,1,0:T(8,128)(2,1)} copy(bf16[16,128,2048]{2,1,0:T(8,128)(2,1)} %get-tuple-element.6) | data formatting | bytes 16777216

commit v4 on v3

--- a/solution.py
+++ b/solution.py
@@ -48,8 +48,10 @@
                             device_id_type=pl.DeviceIdType.MESH)
     own_pos = pltpu.make_async_copy(pos_hbm, pos_buf.at[me], own_sem)
     own_pos.start()
-    for i in range(4):
-        weight_copy(i).start()
+    first_own = pltpu.make_async_copy(
+        x_hbm.at[me * per], x_buf.at[0, pl.ds(pl.multiple_of(my_core * blk, blk), blk)], ld_sem.at[0, my_core])
+    first_own.start()
+    weight_copy(0).start()
     pl.semaphore_wait(barrier, n - 1)
 
     partners = [(0, 1)] + [(dc, fl) for dc in ([1, chips - 1] + list(range(2, chips - 1))) for fl in (0, 1)]
@@ -77,6 +79,8 @@
     for s in range(per):
         for pi in range(n - 1):
             x_copy(pi, s).start()
+    weight_copy(1).start()
+    weight_copy(2).start()
     own_pos.wait()
     for gi, g in enumerate((gq_ref, gk_ref, ga_ref)):
         g_tab[gi:gi + 1, :] = g[...].astype(F32).reshape(1, width)
@@ -159,13 +163,13 @@
         row0 = pl.multiple_of(s * seq + c * ch, ch)
         x = x_buf.at[slot]
         wait_load(slot)
+
+        @pl.when(first)
+        def _():
+            weight_copy(0).wait()
+
+        zero = jnp.zeros((ch, HEAD_DIM), F32)
         tables(s, c)
-
-        @pl.when(first)
-        def _():
-            weight_copy(0).wait()
-
-        zero = jnp.zeros((ch, HEAD_DIM), F32)
         acc = zero
         for j in range(tiles):
             acc = proj_tile(x, wq, q_buf, row0, j, acc)
@@ -184,6 +188,10 @@
         @pl.when(first)
         def _():
             weight_copy(2).wait()
+
+        @pl.when(first)
+        def _():
+            weight_copy(3).start()
 
         prefetch()
 
@@ -251,14 +259,14 @@
                 o_buf[...], wo[:, cols], preferred_element_type=F32).astype(BF16)
 
     def phase(s, carry):
-        lo = jnp.where(s == 0, 0, n_own)
-        start = jnp.where(s == 0, -n_own, 0)
+        start = jnp.where(s == 0, -n_own, jnp.where(s < per, 0, chips - 1))
 
         @pl.when(s == 0)
         def _():
-            load_own(0, 0)
-
-        @pl.when(s > 0)
+            wait_x(0, sib)
+            half_copy(xr_hbm.at[0, sib], 0, 1 - my_core).start()
+
+        @pl.when(jnp.logical_and(s > 0, s < per))
         def _():
             load_other(s, lax.rem(my_chip + offset_of(0), chips), 0)
 
@@ -292,27 +300,33 @@
             weight_copy(3).wait()
 
         def out_step(i, carry):
-            c = jnp.where(i == chips - 1, my_chip, lax.rem(my_chip + offset_of(i), chips))
+            up = lax.rem(my_chip + 1, chips)
+            down = lax.rem(my_chip + chips - 1, chips)
+            own = s == per
+            sq = jnp.where(own, i, s)
+            c = lax.rem(my_chip + offset_of(i), chips)
+            c = jnp.where(i == 0, jnp.minimum(up, down), jnp.where(i == 1, jnp.maximum(up, down), c))
+            c = jnp.where(own, my_chip, c)
             for blk_i in range(chips):
                 @pl.when(c == blk_i)
                 def _():
-                    attend(s, blk_i)
-            out_chunk(s, c)
+                    attend(sq, blk_i)
+            out_chunk(sq, c)
             for core in range(2):
                 mine = jnp.logical_and(c == my_chip, core == my_core)
 
                 @pl.when(mine)
                 def _():
-                    a_local(s).start()
+                    a_local(sq).start()
 
                 @pl.when(jnp.logical_not(mine))
                 def _():
-                    a_copy(s, c, core).start()
+                    a_copy(sq, c, core).start()
             return carry
-        lax.fori_loop(0, chips, out_step, 0)
+        lax.fori_loop(0, jnp.where(s < per, chips - 1, per), out_step, 0)
         return carry
 
-    lax.fori_loop(0, per, phase, 0)
+    lax.fori_loop(0, per + 1, phase, 0)
 
     home = [(0, 1)] + [(dc, fl) for fl in (0, 1) for dc in (chips - 1, 1)] + partners[5:]
 

time: 205 us -> 202 us (0.985)
  the two profiles are of different devices: /device:TPU:83 before, /device:TPU:81 now
where the time goes in v4:
time: 202 us; the launch traced here: 200 us
  Pallas kernels  192 us (95%)
  local copies, waits for them, and re-layouts  8.44 us (4%)
    pallas_call x1, Pallas kernels, exchange_attention(): pl.pallas_call(functools.partial(kernel, n, per, blk, width), out_shape=(...  192 us
    unnamed x1, local copies, waits for them, and re-layouts  8.44 us

profile of v4, /device:TPU:81, one launch (start us, length us, event | category | flops | bytes accessed | tf_op | source)
XLA Modules:
  0.0 200.0 jit_solution(16618291022364018566)
XLA Ops:
  0.0 191.6 %exchange_attention.1 = (bf16[2,8,128,2048]{3,2,1,0:T(8,128)(2,1)}, bf16[16,128,2048]{2,1,0:T(8,128)(2,1)}, bf16[16,128,2048]{2,1,0:T(8,128)(2,1)}) custom-call(bf16[16,128,2048]{2,1,0:T(8,128)(2,1)} %x_hbm.1, s32[16,128]{1,0:T(8,128)} %pos_hbm.1, bf16[2048,2048]{1,0:T(8,128)(2,1)} %wq_hbm.1, bf16[2048,2048]{1,0:T(8,128)(2,1)} %wk_hbm.1, ...), custom_call_target="tpu_custom_call" | custom-call | tf_op jit(solution)/shard_map/exchange_attention/pallas_call | solution.py:418
  191.6 8.4 %copy.12 = bf16[16,128,2048]{2,1,0:T(8,128)(2,1)} copy(bf16[16,128,2048]{2,1,0:T(8,128)(2,1)} %get-tuple-element.6) | data formatting | bytes 16777216
